TPU v7x, 32 devices: a whole 2x2x4 slice. The times are simulated.
32 devices in a mesh: blk: 8 (over y, x, core), col: 4 (over z).
Axes of the slice: x: 2, y: 2, z: 4, core: 2. Of those that a mesh axis runs over, the one named last changes fastest.
Arguments:
- samples: bfloat16 [2048, 768], P('blk'), may hold values from -3 to 3
- targets: float32 [2048, 256], P('blk'), may hold values from -6 to 6
- batch_index: int32 [1024], P('blk'), may hold values from 0 to 255
- centers: bfloat16 [4096, 768], P(('blk', 'col')), may hold values from -3 to 3
- weights: float32 [4096, 256], P(('blk', 'col')), may hold values from -6 to 6
- nystrom_index: int32 [1536], replicated, may hold values from 0 to 4095, as said below
- eigvecs: float32 [1536, 128], replicated, may hold values from -0.15625 to 0.15625
- coefficient: float32 [128], replicated, may hold values from 0.4 to 0.95
Outputs:
- residual: float32 [1024, 256], P(('blk', 'col'))
- new_weights: float32 [4096, 256], P(('blk', 'col'))
Inputs may be any that keep to these rules, and one draw needn't show every extreme that they name: Batch row i is sample row (i // 128) * 256 + batch_index[i]. `nystrom_index`: 1536 distinct center rows.
All inputs are finite; a program needn't handle non-finite values.
Results may differ from a plain program's by a relative error of at most 0.0003.
The roundings to bfloat16 on the way count: a program that leaves them out, or rounds other values in their place, can miss the bound.
Values may be sent and summed in bfloat16 or wider, within the bound.
No kernel may reach another device: no remote copies, remote signals or barrier semaphores. Data moves between devices by JAX's collectives and lax.ppermute only.
A program may use at most 64 MiB of HBM per device.

v0:
```python
import jax
import jax.numpy as jnp
from jax import lax
from jax.sharding import PartitionSpec as P

spread = 1.0
shift_sq = 1.0
step_size = 4.0


def shifted(block, axis, distance):
    devices = range(lax.axis_size(axis))
    route = [((i - distance) % len(devices), i) for i in devices]
    return lax.ppermute(block, axis, route)


def kernel_block(points, centers, center_sq):
    point_sq = jnp.sum(jnp.square(points.astype(jnp.float32)), axis=1, keepdims=True)
    cross = lax.dot_general(
        points, centers, (((1,), (1,)), ((), ())), preferred_element_type=jnp.float32
    )
    dist_sq = point_sq + center_sq[None, :] - 2.0 * cross
    return jnp.exp(-jnp.sqrt(dist_sq + shift_sq) / spread).astype(jnp.bfloat16)


def move_up(points_now):
    return shifted(points_now, "blk", 1)


def pass_up(partial_value):
    return shifted(partial_value, "blk", 1)


def local(samples, targets, batch_index, centers, weights, nystrom_index, eigvecs, coefficient):
    blocks = lax.axis_size("blk")
    columns = lax.axis_size("col")
    my_block = lax.axis_index("blk")
    blk_rows = batch_index.shape[0]
    n_center = centers.shape[0]
    out_width = weights.shape[1]
    points = jnp.take(samples, batch_index, axis=0)
    wanted = jnp.take(targets, batch_index, axis=0)
    center_sq = jnp.sum(jnp.square(centers.astype(jnp.float32)), axis=1)
    weights_low = weights.astype(jnp.bfloat16)
    kernel_store = jnp.zeros((blocks * blk_rows, n_center), jnp.bfloat16)

    def absorb(points_now, partial_value, stored, offset):
        kernel = kernel_block(points_now, centers, center_sq)
        stored = lax.dynamic_update_slice(stored, kernel, (offset, 0))
        return (
            partial_value + jnp.dot(kernel, weights_low, preferred_element_type=jnp.float32),
            stored,
        )

    def walk_step(step_idx, state_now):
        points_now, partial_value, stored = state_now
        partial_value, stored = absorb(
            points_now, partial_value, stored, (my_block - step_idx) % blocks * blk_rows
        )
        return (move_up(points_now), pass_up(partial_value), stored)

    initial = (points, jnp.zeros((blk_rows, out_width), jnp.float32), kernel_store)
    points_now, partial_value, kernel_store = lax.fori_loop(0, blocks - 1, walk_step, initial)
    partial_value, kernel_store = absorb(
        points_now, partial_value, kernel_store, (my_block + 1) % blocks * blk_rows
    )
    partial_value = pass_up(partial_value)
    share_rows = blk_rows // columns
    prediction = lax.psum(partial_value, "col")
    residual_full = prediction - wanted
    gathered = lax.all_gather(residual_full.astype(jnp.bfloat16), "blk", axis=0, tiled=True)
    own_resid = lax.dynamic_slice_in_dim(
        residual_full, lax.axis_index("col") * share_rows, share_rows, 0
    )
    gradient = lax.dot_general(
        kernel_store, gathered, (((0,), (0,)), ((), ())), preferred_element_type=jnp.float32
    )
    first_row = lax.axis_index(("blk", "col")) * n_center
    position = nystrom_index - first_row
    inside = (position >= 0) & (position < n_center)
    position = jnp.where(inside, position, n_center)
    target_row = jnp.minimum(position, n_center - 1)
    picked = jnp.where(inside[:, None], jnp.take(gradient, target_row, axis=0), 0.0)
    highest = lax.Precision.HIGHEST
    local_proj = lax.dot_general(eigvecs, picked, (((0,), (0,)), ((), ())), precision=highest)
    projected = lax.psum(local_proj, ("blk", "col"))
    correction = jnp.dot(eigvecs, coefficient[:, None] * projected, precision=highest)
    adjusted = gradient.at[position].add(-correction, mode="drop")
    return (own_resid, weights - step_size * adjusted)


def solution(mesh):
    in_specs = (
        P("blk", None),
        P("blk", None),
        P("blk"),
        P(("blk", "col"), None),
        P(("blk", "col"), None),
        P(),
        P(),
        P(),
    )
    out_specs = (P(("blk", "col"), None), P(("blk", "col"), None))
    return jax.shard_map(local, mesh=mesh, in_specs=in_specs, out_specs=out_specs, check_vma=False)
```

profile of v0, /device:TPU:0, one launch (start us, length us, event | category | flops | bytes accessed | tf_op | source)
XLA Modules:
  0.0 271.0 jit_solution(4618817647422644272)
XLA Ops:
  7.2 0.8 compare_and_fusion.2
  8.0 0.7 compare_select_fusion.2
  8.7 1.0 multiply_reduce_fusion.2
  9.7 0.9 convert_element_type.36
  10.6 2.0 gather_fusion
  12.7 0.1 broadcast_select_fusion
  12.8 53.1 %while.19 = (s32[]{:T(128)}, bf16[128,768]{1,0:T(8,128)(2,1)S(1)}, f32[128,256]{1,0:T(8,128)S(1)}, bf16[1024,128]{1,0:T(8,128)(2,1)S(1)}, f32[128]{0:T(128)S(1)}...) while((s32[]{:T(128)}, bf16[128,768]{1,0:T(8,128)(2,1)S(1)}, ...), condition=%wide.region_3.4_spmd, body=%wide.region_1.3_spmd.sunk | while | flops 33980304 | bytes 2721664 | solution.py:63
  12.9 0.5 collective-permute-start
  13.4 0.1 multiply_reduce_fusion.4
  13.5 0.3 constant_dynamic-update-slice_fusion.3
  13.8 0.2 convolution_add_fusion.3
  14.0 2.6 collective-permute-start.1
  16.6 4.4 %collective-permute-done.1 = f32[128,256]{1,0:T(8,128)S(1)} collective-permute-done((f32[128,256]{1,0:T(8,128)S(1)}, f32[128,256]{1,0:T(8,128)S(1)}, u32[]{:S(2)}, u32[]{:S(2)}) %collective-permute-start.1) | collective-permute-done | bytes 131104 | tf_op jit(solution)/shard_map/while/body/eval_jaxpr/ppermute | solution.py:14
  21.1 0.1 multiply_reduce_fusion.4
  21.3 0.3 constant_dynamic-update-slice_fusion.3
  21.5 0.2 convolution_add_fusion.3
  21.7 1.5 collective-permute-start.1
  23.2 5.3 %collective-permute-done.1 = f32[128,256]{1,0:T(8,128)S(1)} collective-permute-done((f32[128,256]{1,0:T(8,128)S(1)}, f32[128,256]{1,0:T(8,128)S(1)}, u32[]{:S(2)}, u32[]{:S(2)}) %collective-permute-start.1) | collective-permute-done | bytes 131104 | tf_op jit(solution)/shard_map/while/body/eval_jaxpr/ppermute | solution.py:14
  28.6 0.1 multiply_reduce_fusion.4
  28.8 0.3 constant_dynamic-update-slice_fusion.3
  29.0 0.2 convolution_add_fusion.3
  29.2 0.6 collective-permute-start.1
  29.7 6.2 %collective-permute-done.1 = f32[128,256]{1,0:T(8,128)S(1)} collective-permute-done((f32[128,256]{1,0:T(8,128)S(1)}, f32[128,256]{1,0:T(8,128)S(1)}, u32[]{:S(2)}, u32[]{:S(2)}) %collective-permute-start.1) | collective-permute-done | bytes 131104 | tf_op jit(solution)/shard_map/while/body/eval_jaxpr/ppermute | solution.py:14
  36.0 0.1 collective-permute-start
  36.1 0.1 multiply_reduce_fusion.4
  36.2 0.3 constant_dynamic-update-slice_fusion.3
  36.5 0.2 convolution_add_fusion.3
  36.6 0.1 collective-permute-start.1
  36.7 6.8 %collective-permute-done.1 = f32[128,256]{1,0:T(8,128)S(1)} collective-permute-done((f32[128,256]{1,0:T(8,128)S(1)}, f32[128,256]{1,0:T(8,128)S(1)}, u32[]{:S(2)}, u32[]{:S(2)}) %collective-permute-start.1) | collective-permute-done | bytes 131104 | tf_op jit(solution)/shard_map/while/body/eval_jaxpr/ppermute | solution.py:14
  43.5 0.1 collective-permute-start
  43.6 0.1 multiply_reduce_fusion.4
  43.7 0.3 constant_dynamic-update-slice_fusion.3
  44.0 0.2 convolution_add_fusion.3
  44.1 0.1 collective-permute-start.1
  44.2 6.8 %collective-permute-done.1 = f32[128,256]{1,0:T(8,128)S(1)} collective-permute-done((f32[128,256]{1,0:T(8,128)S(1)}, f32[128,256]{1,0:T(8,128)S(1)}, u32[]{:S(2)}, u32[]{:S(2)}) %collective-permute-start.1) | collective-permute-done | bytes 131104 | tf_op jit(solution)/shard_map/while/body/eval_jaxpr/ppermute | solution.py:14
  51.0 0.1 collective-permute-start
  51.0 0.1 multiply_reduce_fusion.4
  51.2 0.3 constant_dynamic-update-slice_fusion.3
  51.4 0.2 convolution_add_fusion.3
  51.6 0.1 collective-permute-start.1
  51.7 6.8 %collective-permute-done.1 = f32[128,256]{1,0:T(8,128)S(1)} collective-permute-done((f32[128,256]{1,0:T(8,128)S(1)}, f32[128,256]{1,0:T(8,128)S(1)}, u32[]{:S(2)}, u32[]{:S(2)}) %collective-permute-start.1) | collective-permute-done | bytes 131104 | tf_op jit(solution)/shard_map/while/body/eval_jaxpr/ppermute | solution.py:14
  58.4 0.1 collective-permute-start
  58.5 0.1 multiply_reduce_fusion.4
  58.6 0.3 constant_dynamic-update-slice_fusion.3
  58.9 0.2 convolution_add_fusion.3
  59.1 6.8 %collective-permute-done.1 = f32[128,256]{1,0:T(8,128)S(1)} collective-permute-done((f32[128,256]{1,0:T(8,128)S(1)}, f32[128,256]{1,0:T(8,128)S(1)}, u32[]{:S(2)}, u32[]{:S(2)}) %collective-permute-start.1) | collective-permute-done | bytes 131104 | tf_op jit(solution)/shard_map/while/body/eval_jaxpr/ppermute | solution.py:14
  65.9 0.1 multiply_reduce_fusion.1
  66.0 0.3 constant_dynamic-update-slice_fusion.1
  66.3 0.2 convolution_add_fusion.1
  66.5 5.2 %collective-permute-done.2 = f32[128,256]{1,0:T(8,128)S(1)} collective-permute-done((f32[128,256]{1,0:T(8,128)S(1)}, f32[128,256]{1,0:T(8,128)S(1)}, u32[]{:S(2)}, u32[]{:S(2)}) %collective-permute-start.2) | collective-permute-done | bytes 131104 | tf_op jit(solution)/shard_map/ppermute | solution.py:14
  71.8 0.7 copy-done.4
  72.5 0.8 gather_fusion.1
  73.3 35.0 %all-reduce.3.cloned.1.call-done = f32[128,256]{1,0:T(8,128)} async-done(((f32[128,256]{1,0:T(8,128)}), f32[128,256]{1,0:T(8,128)}) %all-reduce.3.cloned.1.call-update) | async-done | bytes 131088 | tf_op jit(solution)/shard_map/psum | solution.py:69
  108.3 1.0 fusion.27
  109.3 9.8 %all_gather.3 = bf16[1024,256]{1,0:T(8,128)(2,1)S(1)} all-gather(bf16[128,256]{1,0:T(8,128)(2,1)S(1)} %get-tuple-element.224), channel_id=1, replica_groups=mesh['blk'=8,'col'=4] {'blk'}, dimensions={0}, use_global_device_ids=true | all-gather | bytes 589824 | tf_op jit(solution)/shard_map/all_gather | solution.py:71
  119.1 0.3 fusion.28
  119.4 3.7 %gather_fusion.2 = f32[1536,256]{1,0:T(8,128)S(1)} fusion(f32[128,256]{1,0:T(8,128)S(1)} %fusion.28, s32[2048]{0:T(1024)S(1)} %pad_clamp_fusion), kind=kCustom, calls=%fused_computation.2 | custom fusion | bytes 3151872 | tf_op jit(solution)/shard_map/jit(_take)/gather | solution.py:83
  123.1 2.6 fusion.10
  125.7 0.6 constant_dynamic-slice_fusion
  126.3 122.8 %all-reduce.5.cloned.1.call-done = f32[128,256]{1,0:T(8,128)} async-done(((f32[128,256]{1,0:T(8,128)}), f32[128,256]{1,0:T(8,128)}) %all-reduce.5.cloned.1.call-update) | async-done | bytes 131088 | tf_op jit(solution)/shard_map/psum | solution.py:86
  249.1 3.6 %fusion.6 = f32[1536,256]{0,1:T(8,128)} fusion(f32[1536,128]{1,0:T(8,128)S(1)} %copy-done, f32[128,256]{1,0:T(8,128)} %all-reduce.5.cloned.1.call-done, f32[128]{0:T(128)S(1)} %copy-done.6), kind=kOutput, calls=%fused_computation.15 | convolution fusion | flops 604405760 | bytes 2490880 | tf_op jit(solution)/shard_map/dot_general | solution.py:87
  252.7 1.9 copy.10
  254.6 8.9 %scatter_fusion = f32[128,256]{1,0:T(8,128)S(1)} fusion(f32[128,256]{1,0:T(8,128)S(1)} %fusion.28, s32[1536]{0:T(1024)S(1)} %compare_select_fusion.1, f32[1536,256]{1,0:T(8,128)S(1)} %copy.10), kind=kCustom, calls=%fused_computation.3 | custom fusion | flops 393216 | bytes 4724736 | tf_op jit(solution)/shard_map/scatter-add | solution.py:88
  263.5 0.7 multiply_subtract_fusion
  (41 shorter events, 0.6 us)
Async XLA Ops:
  7.2 115.9 %copy-start = (f32[1536,128]{1,0:T(8,128)S(1)}, f32[1536,128]{1,0:T(8,128)}, u32[]{:S(2)}) copy-start(f32[1536,128]{1,0:T(8,128)} %param.16) | copy-start | bytes 2359300
  7.2 5.6 %copy-start.3 = (bf16[128,768]{1,0:T(8,128)(2,1)S(1)}, bf16[128,768]{1,0:T(8,128)(2,1)}, u32[]{:S(2)}) copy-start(bf16[128,768]{1,0:T(8,128)(2,1)} %param.13) | copy-start | bytes 589828
  7.2 101.1 %all-reduce.3.cloned.1.call-start = ((), (), s32[]{:S(2)}) async-start(), calls=%async_computation | async-start | bytes 262144 | tf_op jit(solution)/shard_map/psum | solution.py:69
  12.8 53.7 %copy-start.5 = (s32[1536]{0:T(1024)S(1)}, s32[1536]{0:T(1024)}, u32[]{:S(2)}) copy-start(s32[1536]{0:T(1024)} %param.15) | copy-start | bytes 18436
  12.9 8.2 %collective-permute-start = (bf16[128,768]{1,0:T(8,128)(2,1)S(1)}, bf16[128,768]{1,0:T(8,128)(2,1)S(1)}, u32[]{:S(2)}, u32[]{:S(2)}) collective-permute-start(bf16[128,768]{1,0:T(8,128)(2,1)S(1)} %copy.17), channel_id=1, source_target_pairs={{28,0},{0,4},{4,8},{8,12},{12,16},{16,20},{20,24},{24,28},{29,1},{... | collective-permute-start | bytes 589832 | tf_op jit(solution)/shard_map/while/body/eval_jaxpr/ppermute | solution.py:14
  14.0 7.1 %collective-permute-start.1 = (f32[128,256]{1,0:T(8,128)S(1)}, f32[128,256]{1,0:T(8,128)S(1)}, u32[]{:S(2)}, u32[]{:S(2)}) collective-permute-start(f32[128,256]{1,0:T(8,128)S(1)} %convolution_add_fusion.3), channel_id=1, source_target_pairs={{28,0},{0,4},{4,8},{8,12},{12,16},{16,20},{20,24},{24,28},{29,1},{... | collective-permute-start | bytes 393224 | tf_op jit(solution)/shard_map/while/body/eval_jaxpr/ppermute | solution.py:14
  21.1 7.5 %collective-permute-start = (bf16[128,768]{1,0:T(8,128)(2,1)S(1)}, bf16[128,768]{1,0:T(8,128)(2,1)S(1)}, u32[]{:S(2)}, u32[]{:S(2)}) collective-permute-start(bf16[128,768]{1,0:T(8,128)(2,1)S(1)} %copy.17), channel_id=1, source_target_pairs={{28,0},{0,4},{4,8},{8,12},{12,16},{16,20},{20,24},{24,28},{29,1},{... | collective-permute-start | bytes 589832 | tf_op jit(solution)/shard_map/while/body/eval_jaxpr/ppermute | solution.py:14
  21.7 6.8 %collective-permute-start.1 = (f32[128,256]{1,0:T(8,128)S(1)}, f32[128,256]{1,0:T(8,128)S(1)}, u32[]{:S(2)}, u32[]{:S(2)}) collective-permute-start(f32[128,256]{1,0:T(8,128)S(1)} %convolution_add_fusion.3), channel_id=1, source_target_pairs={{28,0},{0,4},{4,8},{8,12},{12,16},{16,20},{20,24},{24,28},{29,1},{... | collective-permute-start | bytes 393224 | tf_op jit(solution)/shard_map/while/body/eval_jaxpr/ppermute | solution.py:14
  28.5 7.5 %collective-permute-start = (bf16[128,768]{1,0:T(8,128)(2,1)S(1)}, bf16[128,768]{1,0:T(8,128)(2,1)S(1)}, u32[]{:S(2)}, u32[]{:S(2)}) collective-permute-start(bf16[128,768]{1,0:T(8,128)(2,1)S(1)} %copy.17), channel_id=1, source_target_pairs={{28,0},{0,4},{4,8},{8,12},{12,16},{16,20},{20,24},{24,28},{29,1},{... | collective-permute-start | bytes 589832 | tf_op jit(solution)/shard_map/while/body/eval_jaxpr/ppermute | solution.py:14
  29.2 6.8 %collective-permute-start.1 = (f32[128,256]{1,0:T(8,128)S(1)}, f32[128,256]{1,0:T(8,128)S(1)}, u32[]{:S(2)}, u32[]{:S(2)}) collective-permute-start(f32[128,256]{1,0:T(8,128)S(1)} %convolution_add_fusion.3), channel_id=1, source_target_pairs={{28,0},{0,4},{4,8},{8,12},{12,16},{16,20},{20,24},{24,28},{29,1},{... | collective-permute-start | bytes 393224 | tf_op jit(solution)/shard_map/while/body/eval_jaxpr/ppermute | solution.py:14
  36.0 7.5 %collective-permute-start = (bf16[128,768]{1,0:T(8,128)(2,1)S(1)}, bf16[128,768]{1,0:T(8,128)(2,1)S(1)}, u32[]{:S(2)}, u32[]{:S(2)}) collective-permute-start(bf16[128,768]{1,0:T(8,128)(2,1)S(1)} %copy.17), channel_id=1, source_target_pairs={{28,0},{0,4},{4,8},{8,12},{12,16},{16,20},{20,24},{24,28},{29,1},{... | collective-permute-start | bytes 589832 | tf_op jit(solution)/shard_map/while/body/eval_jaxpr/ppermute | solution.py:14
  36.6 6.8 %collective-permute-start.1 = (f32[128,256]{1,0:T(8,128)S(1)}, f32[128,256]{1,0:T(8,128)S(1)}, u32[]{:S(2)}, u32[]{:S(2)}) collective-permute-start(f32[128,256]{1,0:T(8,128)S(1)} %convolution_add_fusion.3), channel_id=1, source_target_pairs={{28,0},{0,4},{4,8},{8,12},{12,16},{16,20},{20,24},{24,28},{29,1},{... | collective-permute-start | bytes 393224 | tf_op jit(solution)/shard_map/while/body/eval_jaxpr/ppermute | solution.py:14
  43.5 7.5 %collective-permute-start = (bf16[128,768]{1,0:T(8,128)(2,1)S(1)}, bf16[128,768]{1,0:T(8,128)(2,1)S(1)}, u32[]{:S(2)}, u32[]{:S(2)}) collective-permute-start(bf16[128,768]{1,0:T(8,128)(2,1)S(1)} %copy.17), channel_id=1, source_target_pairs={{28,0},{0,4},{4,8},{8,12},{12,16},{16,20},{20,24},{24,28},{29,1},{... | collective-permute-start | bytes 589832 | tf_op jit(solution)/shard_map/while/body/eval_jaxpr/ppermute | solution.py:14
  44.1 6.8 %collective-permute-start.1 = (f32[128,256]{1,0:T(8,128)S(1)}, f32[128,256]{1,0:T(8,128)S(1)}, u32[]{:S(2)}, u32[]{:S(2)}) collective-permute-start(f32[128,256]{1,0:T(8,128)S(1)} %convolution_add_fusion.3), channel_id=1, source_target_pairs={{28,0},{0,4},{4,8},{8,12},{12,16},{16,20},{20,24},{24,28},{29,1},{... | collective-permute-start | bytes 393224 | tf_op jit(solution)/shard_map/while/body/eval_jaxpr/ppermute | solution.py:14
  51.0 7.5 %collective-permute-start = (bf16[128,768]{1,0:T(8,128)(2,1)S(1)}, bf16[128,768]{1,0:T(8,128)(2,1)S(1)}, u32[]{:S(2)}, u32[]{:S(2)}) collective-permute-start(bf16[128,768]{1,0:T(8,128)(2,1)S(1)} %copy.17), channel_id=1, source_target_pairs={{28,0},{0,4},{4,8},{8,12},{12,16},{16,20},{20,24},{24,28},{29,1},{... | collective-permute-start | bytes 589832 | tf_op jit(solution)/shard_map/while/body/eval_jaxpr/ppermute | solution.py:14
  51.6 6.8 %collective-permute-start.1 = (f32[128,256]{1,0:T(8,128)S(1)}, f32[128,256]{1,0:T(8,128)S(1)}, u32[]{:S(2)}, u32[]{:S(2)}) collective-permute-start(f32[128,256]{1,0:T(8,128)S(1)} %convolution_add_fusion.3), channel_id=1, source_target_pairs={{28,0},{0,4},{4,8},{8,12},{12,16},{16,20},{20,24},{24,28},{29,1},{... | collective-permute-start | bytes 393224 | tf_op jit(solution)/shard_map/while/body/eval_jaxpr/ppermute | solution.py:14
  58.4 7.5 %collective-permute-start = (bf16[128,768]{1,0:T(8,128)(2,1)S(1)}, bf16[128,768]{1,0:T(8,128)(2,1)S(1)}, u32[]{:S(2)}, u32[]{:S(2)}) collective-permute-start(bf16[128,768]{1,0:T(8,128)(2,1)S(1)} %copy.17), channel_id=1, source_target_pairs={{28,0},{0,4},{4,8},{8,12},{12,16},{16,20},{20,24},{24,28},{29,1},{... | collective-permute-start | bytes 589832 | tf_op jit(solution)/shard_map/while/body/eval_jaxpr/ppermute | solution.py:14
  59.1 6.8 %collective-permute-start.1 = (f32[128,256]{1,0:T(8,128)S(1)}, f32[128,256]{1,0:T(8,128)S(1)}, u32[]{:S(2)}, u32[]{:S(2)}) collective-permute-start(f32[128,256]{1,0:T(8,128)S(1)} %convolution_add_fusion.3), channel_id=1, source_target_pairs={{28,0},{0,4},{4,8},{8,12},{12,16},{16,20},{20,24},{24,28},{29,1},{... | collective-permute-start | bytes 393224 | tf_op jit(solution)/shard_map/while/body/eval_jaxpr/ppermute | solution.py:14
  65.9 6.6 %copy-start.1 = (f32[256,256]{1,0:T(8,128)S(1)}, f32[256,256]{1,0:T(8,128)}, u32[]{:S(2)}) copy-start(f32[256,256]{1,0:T(8,128)} %param.11) | copy-start | bytes 786436
  66.4 5.3 %collective-permute-start.2 = (f32[128,256]{1,0:T(8,128)S(1)}, f32[128,256]{1,0:T(8,128)S(1)}, u32[]{:S(2)}, u32[]{:S(2)}) collective-permute-start(f32[128,256]{1,0:T(8,128)S(1)} %convolution_add_fusion.1), channel_id=1, source_target_pairs={{28,0},{0,4},{4,8},{8,12},{12,16},{16,20},{20,24},{24,28},{29,1},{... | collective-permute-start | bytes 393224 | tf_op jit(solution)/shard_map/ppermute | solution.py:14
  71.8 0.7 copy-start.4
  72.4 176.6 %all-reduce.5.cloned.1.call-start = ((), (), s32[]{:S(2)}) async-start(), calls=%async_computation.1 | async-start | bytes 262144 | tf_op jit(solution)/shard_map/psum | solution.py:86
  123.1 126.0 %copy-start.6 = (f32[128]{0:T(128)S(1)}, f32[128]{0:T(128)}, u32[]{:S(2)}) copy-start(f32[128]{0:T(128)} %param.17) | copy-start | bytes 1540
  254.6 8.9 %copy-start.2 = (f32[128,256]{1,0:T(8,128)S(1)}, f32[128,256]{1,0:T(8,128)}, u32[]{:S(2)}) copy-start(f32[128,256]{1,0:T(8,128)} %param.14) | copy-start | bytes 393220
Sparse Core Ops, SparseCore 0:
  72.6 35.7 all-reduce.2
  125.8 123.2 all-reduce.4
where the time goes:
time: 271 us
  waiting for transfers between devices  206 us (76%)
  other arithmetic  15 us (6%)
  between operations  14.3 us (5%)
  blocking collectives  9.79 us (4%)
  local copies, waits for them, and re-layouts  9.77 us (4%)
  matrix products  9.7 us (4%)
  starting transfers between devices  5.97 us (2%)
    psum x1, waiting for transfers between devices, local(): projected = lax.psum(local_proj, ('blk', 'col'))  123 us
    ppermute x15, waiting for transfers between devices, shifted(): return lax.ppermute(block, axis, route)  48.3 us
    psum x1, waiting for transfers between devices, local(): prediction = lax.psum(partial_value, 'col')  35 us
    all_gather x1, blocking collectives, local(): lax.all_gather(residual_full.astype(jnp.bfloat16), 'blk', axis=0, tiled=T...  9.79 us
    scatter-add x1, other arithmetic, local(): adjusted = gradient.at[position].add(-correction, mode='drop')  8.88 us
    ppermute x15, starting transfers between devices, shifted(): return lax.ppermute(block, axis, route)  5.89 us
  transfers between devices with their start and end apart: 17, of which 10 were waited for; matrix products, arithmetic and copies ran while one was open for 2% of the time, Pallas kernels for 0%

commit v1 on v0

--- a/solution.py
+++ b/solution.py
@@ -66,7 +66,7 @@
     )
     partial_value = pass_up(partial_value)
     share_rows = blk_rows // columns
-    prediction = lax.psum(partial_value, "col")
+    prediction = jnp.sum(lax.all_gather(partial_value, "col"), axis=0)
     residual_full = prediction - wanted
     gathered = lax.all_gather(residual_full.astype(jnp.bfloat16), "blk", axis=0, tiled=True)
     own_resid = lax.dynamic_slice_in_dim(

time: 271 us -> 251 us (0.926)
  waiting for transfers between devices: 206 us -> 171 us
  blocking collectives: 9.79 us -> 26.7 us
    psum x1 -> x0, waiting for transfers between devices: 35 us -> none  [local(): prediction = lax.psum(partial_value, 'col')]
    all_gather x0 -> x1, blocking collectives: none -> 16.9 us  [local(): prediction = jnp.sum(lax.all_gather(partial_value, 'col'), axis=0)]
  transfers between devices with their start and end apart: 17 -> 16, of which waited for: 10 -> 9; matrix products, arithmetic and copies ran while one was open for 2% -> 2% of each run, Pallas kernels for 0% -> 0%
where the time goes in v1:
time: 251 us
  waiting for transfers between devices  171 us (68%)
  blocking collectives  26.7 us (11%)
  between operations  14.2 us (6%)
  other arithmetic  14.1 us (6%)
  matrix products  9.68 us (4%)
  local copies, waits for them, and re-layouts  9.4 us (4%)
  starting transfers between devices  5.92 us (2%)
    psum x1, waiting for transfers between devices, local(): projected = lax.psum(local_proj, ('blk', 'col'))  123 us
    ppermute x15, waiting for transfers between devices, shifted(): return lax.ppermute(block, axis, route)  47.2 us
    all_gather x1, blocking collectives, local(): prediction = jnp.sum(lax.all_gather(partial_value, 'col'), axis=0)  16.9 us
    all_gather x1, blocking collectives, local(): lax.all_gather(residual_full.astype(jnp.bfloat16), 'blk', axis=0, tiled=T...  9.85 us
    scatter-add x1, other arithmetic, local(): adjusted = gradient.at[position].add(-correction, mode='drop')  8.88 us
    ppermute x15, starting transfers between devices, shifted(): return lax.ppermute(block, axis, route)  5.88 us
  transfers between devices with their start and end apart: 16, of which 9 were waited for; matrix products, arithmetic and copies ran while one was open for 2% of the time, Pallas kernels for 0%

profile of v1, /device:TPU:0, one launch (start us, length us, event | category | flops | bytes accessed | tf_op | source)
XLA Modules:
  0.0 251.2 jit_solution(10583542001570277191)
XLA Ops:
  7.2 0.8 compare_and_fusion.2
  8.0 0.7 compare_select_fusion.2
  8.7 1.0 multiply_reduce_fusion.2
  9.7 0.9 convert_element_type.36
  10.6 2.0 gather_fusion
  12.7 0.1 broadcast_select_fusion
  12.8 53.1 %while.19 = (s32[]{:T(128)}, bf16[128,768]{1,0:T(8,128)(2,1)S(1)}, f32[128,256]{1,0:T(8,128)S(1)}, bf16[1024,128]{1,0:T(8,128)(2,1)S(1)}, f32[128]{0:T(128)S(1)}...) while((s32[]{:T(128)}, bf16[128,768]{1,0:T(8,128)(2,1)S(1)}, ...), condition=%wide.region_3.4_spmd, body=%wide.region_1.3_spmd.sunk | while | flops 33980304 | bytes 2721664 | solution.py:63
  12.9 0.5 collective-permute-start
  13.4 0.1 multiply_reduce_fusion.4
  13.5 0.3 constant_dynamic-update-slice_fusion.3
  13.8 0.2 convolution_add_fusion.3
  14.0 2.6 %collective-permute-start.1 = (f32[128,256]{1,0:T(8,128)S(1)}, f32[128,256]{1,0:T(8,128)S(1)}, u32[]{:S(2)}, u32[]{:S(2)}) collective-permute-start(f32[128,256]{1,0:T(8,128)S(1)} %convolution_add_fusion.3), channel_id=1, source_target_pairs={{28,0},{0,4},{4,8},{8,12},{12,16},{16,20},{20,24},{24,28},{29,1},{... | collective-permute-start | bytes 393224 | tf_op jit(solution)/shard_map/while/body/eval_jaxpr/ppermute | solution.py:14
  16.6 4.4 %collective-permute-done.1 = f32[128,256]{1,0:T(8,128)S(1)} collective-permute-done((f32[128,256]{1,0:T(8,128)S(1)}, f32[128,256]{1,0:T(8,128)S(1)}, u32[]{:S(2)}, u32[]{:S(2)}) %collective-permute-start.1) | collective-permute-done | bytes 131104 | tf_op jit(solution)/shard_map/while/body/eval_jaxpr/ppermute | solution.py:14
  21.1 0.1 collective-permute-start
  21.1 0.1 multiply_reduce_fusion.4
  21.3 0.3 constant_dynamic-update-slice_fusion.3
  21.5 0.2 convolution_add_fusion.3
  21.7 1.5 collective-permute-start.1
  23.2 5.3 %collective-permute-done.1 = f32[128,256]{1,0:T(8,128)S(1)} collective-permute-done((f32[128,256]{1,0:T(8,128)S(1)}, f32[128,256]{1,0:T(8,128)S(1)}, u32[]{:S(2)}, u32[]{:S(2)}) %collective-permute-start.1) | collective-permute-done | bytes 131104 | tf_op jit(solution)/shard_map/while/body/eval_jaxpr/ppermute | solution.py:14
  28.5 0.1 collective-permute-start
  28.6 0.1 multiply_reduce_fusion.4
  28.7 0.3 constant_dynamic-update-slice_fusion.3
  29.0 0.2 convolution_add_fusion.3
  29.2 0.6 collective-permute-start.1
  29.7 6.2 %collective-permute-done.1 = f32[128,256]{1,0:T(8,128)S(1)} collective-permute-done((f32[128,256]{1,0:T(8,128)S(1)}, f32[128,256]{1,0:T(8,128)S(1)}, u32[]{:S(2)}, u32[]{:S(2)}) %collective-permute-start.1) | collective-permute-done | bytes 131104 | tf_op jit(solution)/shard_map/while/body/eval_jaxpr/ppermute | solution.py:14
  36.0 0.1 collective-permute-start
  36.1 0.1 multiply_reduce_fusion.4
  36.2 0.3 constant_dynamic-update-slice_fusion.3
  36.5 0.2 convolution_add_fusion.3
  36.6 0.1 collective-permute-start.1
  36.7 6.8 %collective-permute-done.1 = f32[128,256]{1,0:T(8,128)S(1)} collective-permute-done((f32[128,256]{1,0:T(8,128)S(1)}, f32[128,256]{1,0:T(8,128)S(1)}, u32[]{:S(2)}, u32[]{:S(2)}) %collective-permute-start.1) | collective-permute-done | bytes 131104 | tf_op jit(solution)/shard_map/while/body/eval_jaxpr/ppermute | solution.py:14
  43.5 0.1 collective-permute-start
  43.6 0.1 multiply_reduce_fusion.4
  43.7 0.3 constant_dynamic-update-slice_fusion.3
  44.0 0.2 convolution_add_fusion.3
  44.1 0.1 collective-permute-start.1
  44.2 6.8 %collective-permute-done.1 = f32[128,256]{1,0:T(8,128)S(1)} collective-permute-done((f32[128,256]{1,0:T(8,128)S(1)}, f32[128,256]{1,0:T(8,128)S(1)}, u32[]{:S(2)}, u32[]{:S(2)}) %collective-permute-start.1) | collective-permute-done | bytes 131104 | tf_op jit(solution)/shard_map/while/body/eval_jaxpr/ppermute | solution.py:14
  51.0 0.1 collective-permute-start
  51.0 0.1 multiply_reduce_fusion.4
  51.2 0.3 constant_dynamic-update-slice_fusion.3
  51.4 0.2 convolution_add_fusion.3
  51.7 6.8 %collective-permute-done.1 = f32[128,256]{1,0:T(8,128)S(1)} collective-permute-done((f32[128,256]{1,0:T(8,128)S(1)}, f32[128,256]{1,0:T(8,128)S(1)}, u32[]{:S(2)}, u32[]{:S(2)}) %collective-permute-start.1) | collective-permute-done | bytes 131104 | tf_op jit(solution)/shard_map/while/body/eval_jaxpr/ppermute | solution.py:14
  58.5 0.1 multiply_reduce_fusion.4
  58.6 0.3 constant_dynamic-update-slice_fusion.3
  58.9 0.1 convolution_add_fusion.3
  59.1 6.8 %collective-permute-done.1 = f32[128,256]{1,0:T(8,128)S(1)} collective-permute-done((f32[128,256]{1,0:T(8,128)S(1)}, f32[128,256]{1,0:T(8,128)S(1)}, u32[]{:S(2)}, u32[]{:S(2)}) %collective-permute-start.1) | collective-permute-done | bytes 131104 | tf_op jit(solution)/shard_map/while/body/eval_jaxpr/ppermute | solution.py:14
  65.9 0.1 multiply_reduce_fusion.1
  66.0 0.3 constant_dynamic-update-slice_fusion.1
  66.3 0.2 convolution_add_fusion.1
  66.5 0.3 copy-done.1
  66.8 0.8 gather_fusion.1
  67.6 4.2 %collective-permute-done.2 = f32[128,256]{1,0:T(8,128)S(1)} collective-permute-done((f32[128,256]{1,0:T(8,128)S(1)}, f32[128,256]{1,0:T(8,128)S(1)}, u32[]{:S(2)}, u32[]{:S(2)}) %collective-permute-start.2) | collective-permute-done | bytes 131104 | tf_op jit(solution)/shard_map/ppermute | solution.py:14
  71.8 16.9 %all-gather = f32[512,256]{1,0:T(8,128)S(1)} all-gather(f32[128,256]{1,0:T(8,128)S(1)} %collective-permute-done.2), channel_id=2, replica_groups=mesh['blk'=8,'col'=4] {'col'}, dimensions={0}, use_global_device_ids=true | all-gather | bytes 655360 | tf_op jit(solution)/shard_map/all_gather | solution.py:69
  88.7 0.1 fusion.27
  88.8 9.9 %all_gather.11 = bf16[1024,256]{1,0:T(8,128)(2,1)S(1)} all-gather(bf16[128,256]{1,0:T(8,128)(2,1)S(1)} %get-tuple-element.224), channel_id=1, replica_groups=mesh['blk'=8,'col'=4] {'blk'}, dimensions={0}, use_global_device_ids=true | all-gather | bytes 589824 | tf_op jit(solution)/shard_map/all_gather | solution.py:71
  98.6 0.3 fusion.28
  98.9 3.7 %gather_fusion.2 = f32[1536,256]{1,0:T(8,128)S(1)} fusion(f32[128,256]{1,0:T(8,128)S(1)} %fusion.28, s32[2048]{0:T(1024)S(1)} %pad_clamp_fusion), kind=kCustom, calls=%fused_computation.2 | custom fusion | bytes 3151872 | tf_op jit(solution)/shard_map/jit(_take)/gather | solution.py:83
  102.6 2.6 %fusion.10 = f32[128,256]{1,0:T(8,128)} fusion(f32[1536,128]{1,0:T(8,128)S(1)} %copy-done, f32[1536,256]{1,0:T(8,128)S(1)} %gather_fusion.2, pred[1536]{0:T(1024)(128)(4,1)S(1)} %get-tuple-element.222, pred[1536]{0:T(1024)(128)(4,1)S(1)} %get-tuple-element.228), kind=kOutput, calls=%fused_computation.19 | convolution fusion | flops 604766208 | bytes 2493440 | tf_op jit(solution)/shard_map/dot_general | solution.py:85
  105.2 0.6 constant_dynamic-slice_fusion
  105.8 123.5 %all-reduce.2.cloned.1.call-done = f32[128,256]{1,0:T(8,128)} async-done(((f32[128,256]{1,0:T(8,128)}), f32[128,256]{1,0:T(8,128)}) %all-reduce.2.cloned.1.call-update) | async-done | bytes 131088 | tf_op jit(solution)/shard_map/psum | solution.py:86
  229.3 3.6 %fusion.6 = f32[1536,256]{0,1:T(8,128)} fusion(f32[1536,128]{1,0:T(8,128)S(1)} %copy-done, f32[128,256]{1,0:T(8,128)} %all-reduce.2.cloned.1.call-done, f32[128]{0:T(128)S(1)} %copy-done.5), kind=kOutput, calls=%fused_computation.15 | convolution fusion | flops 604405760 | bytes 2490880 | tf_op jit(solution)/shard_map/dot_general | solution.py:87
  232.8 1.9 copy.10
  234.7 8.9 %scatter_fusion = f32[128,256]{1,0:T(8,128)S(1)} fusion(f32[128,256]{1,0:T(8,128)S(1)} %fusion.28, s32[1536]{0:T(1024)S(1)} %compare_select_fusion.1, f32[1536,256]{1,0:T(8,128)S(1)} %copy.10), kind=kCustom, calls=%fused_computation.3 | custom fusion | flops 393216 | bytes 4724736 | tf_op jit(solution)/shard_map/scatter-add | solution.py:88
  243.6 0.7 multiply_subtract_fusion
  (38 shorter events, 0.6 us)
Async XLA Ops:
  7.2 95.4 %copy-start = (f32[1536,128]{1,0:T(8,128)S(1)}, f32[1536,128]{1,0:T(8,128)}, u32[]{:S(2)}) copy-start(f32[1536,128]{1,0:T(8,128)} %param.16) | copy-start | bytes 2359300
  7.2 5.6 %copy-start.3 = (bf16[128,768]{1,0:T(8,128)(2,1)S(1)}, bf16[128,768]{1,0:T(8,128)(2,1)}, u32[]{:S(2)}) copy-start(bf16[128,768]{1,0:T(8,128)(2,1)} %param.13) | copy-start | bytes 589828
  7.2 222.1 %all-reduce.2.cloned.1.call-start = ((), (), s32[]{:S(2)}) async-start(), calls=%async_computation | async-start | bytes 262144 | tf_op jit(solution)/shard_map/psum | solution.py:86
  12.8 53.7 %copy-start.4 = (s32[1536]{0:T(1024)S(1)}, s32[1536]{0:T(1024)}, u32[]{:S(2)}) copy-start(s32[1536]{0:T(1024)} %param.15) | copy-start | bytes 18436
  12.9 8.2 %collective-permute-start = (bf16[128,768]{1,0:T(8,128)(2,1)S(1)}, bf16[128,768]{1,0:T(8,128)(2,1)S(1)}, u32[]{:S(2)}, u32[]{:S(2)}) collective-permute-start(bf16[128,768]{1,0:T(8,128)(2,1)S(1)} %copy.17), channel_id=1, source_target_pairs={{28,0},{0,4},{4,8},{8,12},{12,16},{16,20},{20,24},{24,28},{29,1},{... | collective-permute-start | bytes 589832 | tf_op jit(solution)/shard_map/while/body/eval_jaxpr/ppermute | solution.py:14
  14.0 7.1 %collective-permute-start.1 = (f32[128,256]{1,0:T(8,128)S(1)}, f32[128,256]{1,0:T(8,128)S(1)}, u32[]{:S(2)}, u32[]{:S(2)}) collective-permute-start(f32[128,256]{1,0:T(8,128)S(1)} %convolution_add_fusion.3), channel_id=1, source_target_pairs={{28,0},{0,4},{4,8},{8,12},{12,16},{16,20},{20,24},{24,28},{29,1},{... | collective-permute-start | bytes 393224 | tf_op jit(solution)/shard_map/while/body/eval_jaxpr/ppermute | solution.py:14
  21.1 7.5 %collective-permute-start = (bf16[128,768]{1,0:T(8,128)(2,1)S(1)}, bf16[128,768]{1,0:T(8,128)(2,1)S(1)}, u32[]{:S(2)}, u32[]{:S(2)}) collective-permute-start(bf16[128,768]{1,0:T(8,128)(2,1)S(1)} %copy.17), channel_id=1, source_target_pairs={{28,0},{0,4},{4,8},{8,12},{12,16},{16,20},{20,24},{24,28},{29,1},{... | collective-permute-start | bytes 589832 | tf_op jit(solution)/shard_map/while/body/eval_jaxpr/ppermute | solution.py:14
  21.7 6.8 %collective-permute-start.1 = (f32[128,256]{1,0:T(8,128)S(1)}, f32[128,256]{1,0:T(8,128)S(1)}, u32[]{:S(2)}, u32[]{:S(2)}) collective-permute-start(f32[128,256]{1,0:T(8,128)S(1)} %convolution_add_fusion.3), channel_id=1, source_target_pairs={{28,0},{0,4},{4,8},{8,12},{12,16},{16,20},{20,24},{24,28},{29,1},{... | collective-permute-start | bytes 393224 | tf_op jit(solution)/shard_map/while/body/eval_jaxpr/ppermute | solution.py:14
  28.5 7.5 %collective-permute-start = (bf16[128,768]{1,0:T(8,128)(2,1)S(1)}, bf16[128,768]{1,0:T(8,128)(2,1)S(1)}, u32[]{:S(2)}, u32[]{:S(2)}) collective-permute-start(bf16[128,768]{1,0:T(8,128)(2,1)S(1)} %copy.17), channel_id=1, source_target_pairs={{28,0},{0,4},{4,8},{8,12},{12,16},{16,20},{20,24},{24,28},{29,1},{... | collective-permute-start | bytes 589832 | tf_op jit(solution)/shard_map/while/body/eval_jaxpr/ppermute | solution.py:14
  29.2 6.8 %collective-permute-start.1 = (f32[128,256]{1,0:T(8,128)S(1)}, f32[128,256]{1,0:T(8,128)S(1)}, u32[]{:S(2)}, u32[]{:S(2)}) collective-permute-start(f32[128,256]{1,0:T(8,128)S(1)} %convolution_add_fusion.3), channel_id=1, source_target_pairs={{28,0},{0,4},{4,8},{8,12},{12,16},{16,20},{20,24},{24,28},{29,1},{... | collective-permute-start | bytes 393224 | tf_op jit(solution)/shard_map/while/body/eval_jaxpr/ppermute | solution.py:14
  36.0 7.5 %collective-permute-start = (bf16[128,768]{1,0:T(8,128)(2,1)S(1)}, bf16[128,768]{1,0:T(8,128)(2,1)S(1)}, u32[]{:S(2)}, u32[]{:S(2)}) collective-permute-start(bf16[128,768]{1,0:T(8,128)(2,1)S(1)} %copy.17), channel_id=1, source_target_pairs={{28,0},{0,4},{4,8},{8,12},{12,16},{16,20},{20,24},{24,28},{29,1},{... | collective-permute-start | bytes 589832 | tf_op jit(solution)/shard_map/while/body/eval_jaxpr/ppermute | solution.py:14
  36.6 6.8 %collective-permute-start.1 = (f32[128,256]{1,0:T(8,128)S(1)}, f32[128,256]{1,0:T(8,128)S(1)}, u32[]{:S(2)}, u32[]{:S(2)}) collective-permute-start(f32[128,256]{1,0:T(8,128)S(1)} %convolution_add_fusion.3), channel_id=1, source_target_pairs={{28,0},{0,4},{4,8},{8,12},{12,16},{16,20},{20,24},{24,28},{29,1},{... | collective-permute-start | bytes 393224 | tf_op jit(solution)/shard_map/while/body/eval_jaxpr/ppermute | solution.py:14
  43.5 7.5 %collective-permute-start = (bf16[128,768]{1,0:T(8,128)(2,1)S(1)}, bf16[128,768]{1,0:T(8,128)(2,1)S(1)}, u32[]{:S(2)}, u32[]{:S(2)}) collective-permute-start(bf16[128,768]{1,0:T(8,128)(2,1)S(1)} %copy.17), channel_id=1, source_target_pairs={{28,0},{0,4},{4,8},{8,12},{12,16},{16,20},{20,24},{24,28},{29,1},{... | collective-permute-start | bytes 589832 | tf_op jit(solution)/shard_map/while/body/eval_jaxpr/ppermute | solution.py:14
  44.1 6.8 %collective-permute-start.1 = (f32[128,256]{1,0:T(8,128)S(1)}, f32[128,256]{1,0:T(8,128)S(1)}, u32[]{:S(2)}, u32[]{:S(2)}) collective-permute-start(f32[128,256]{1,0:T(8,128)S(1)} %convolution_add_fusion.3), channel_id=1, source_target_pairs={{28,0},{0,4},{4,8},{8,12},{12,16},{16,20},{20,24},{24,28},{29,1},{... | collective-permute-start | bytes 393224 | tf_op jit(solution)/shard_map/while/body/eval_jaxpr/ppermute | solution.py:14
  51.0 7.5 %collective-permute-start = (bf16[128,768]{1,0:T(8,128)(2,1)S(1)}, bf16[128,768]{1,0:T(8,128)(2,1)S(1)}, u32[]{:S(2)}, u32[]{:S(2)}) collective-permute-start(bf16[128,768]{1,0:T(8,128)(2,1)S(1)} %copy.17), channel_id=1, source_target_pairs={{28,0},{0,4},{4,8},{8,12},{12,16},{16,20},{20,24},{24,28},{29,1},{... | collective-permute-start | bytes 589832 | tf_op jit(solution)/shard_map/while/body/eval_jaxpr/ppermute | solution.py:14
  51.6 6.8 %collective-permute-start.1 = (f32[128,256]{1,0:T(8,128)S(1)}, f32[128,256]{1,0:T(8,128)S(1)}, u32[]{:S(2)}, u32[]{:S(2)}) collective-permute-start(f32[128,256]{1,0:T(8,128)S(1)} %convolution_add_fusion.3), channel_id=1, source_target_pairs={{28,0},{0,4},{4,8},{8,12},{12,16},{16,20},{20,24},{24,28},{29,1},{... | collective-permute-start | bytes 393224 | tf_op jit(solution)/shard_map/while/body/eval_jaxpr/ppermute | solution.py:14
  58.4 7.5 %collective-permute-start = (bf16[128,768]{1,0:T(8,128)(2,1)S(1)}, bf16[128,768]{1,0:T(8,128)(2,1)S(1)}, u32[]{:S(2)}, u32[]{:S(2)}) collective-permute-start(bf16[128,768]{1,0:T(8,128)(2,1)S(1)} %copy.17), channel_id=1, source_target_pairs={{28,0},{0,4},{4,8},{8,12},{12,16},{16,20},{20,24},{24,28},{29,1},{... | collective-permute-start | bytes 589832 | tf_op jit(solution)/shard_map/while/body/eval_jaxpr/ppermute | solution.py:14
  59.1 6.8 %collective-permute-start.1 = (f32[128,256]{1,0:T(8,128)S(1)}, f32[128,256]{1,0:T(8,128)S(1)}, u32[]{:S(2)}, u32[]{:S(2)}) collective-permute-start(f32[128,256]{1,0:T(8,128)S(1)} %convolution_add_fusion.3), channel_id=1, source_target_pairs={{28,0},{0,4},{4,8},{8,12},{12,16},{16,20},{20,24},{24,28},{29,1},{... | collective-permute-start | bytes 393224 | tf_op jit(solution)/shard_map/while/body/eval_jaxpr/ppermute | solution.py:14
  65.9 1.0 copy-start.1
  66.4 5.3 %collective-permute-start.2 = (f32[128,256]{1,0:T(8,128)S(1)}, f32[128,256]{1,0:T(8,128)S(1)}, u32[]{:S(2)}, u32[]{:S(2)}) collective-permute-start(f32[128,256]{1,0:T(8,128)S(1)} %convolution_add_fusion.1), channel_id=1, source_target_pairs={{28,0},{0,4},{4,8},{8,12},{12,16},{16,20},{20,24},{24,28},{29,1},{... | collective-permute-start | bytes 393224 | tf_op jit(solution)/shard_map/ppermute | solution.py:14
  102.6 126.7 %copy-start.5 = (f32[128]{0:T(128)S(1)}, f32[128]{0:T(128)}, u32[]{:S(2)}) copy-start(f32[128]{0:T(128)} %param.17) | copy-start | bytes 1540
  234.7 8.9 %copy-start.2 = (f32[128,256]{1,0:T(8,128)S(1)}, f32[128,256]{1,0:T(8,128)}, u32[]{:S(2)}) copy-start(f32[128,256]{1,0:T(8,128)} %param.14) | copy-start | bytes 393220
Sparse Core Ops, SparseCore 0:
  105.3 123.9 all-reduce.1
